TPU v7x, 256 devices: a whole 4x4x8 slice. The times are simulated.
256 devices in a mesh: block: 8 (over z_lo, x_lo, core), span: 4 (over z_hi), model: 8 (over y, x_hi).
Axes of the slice: x: 4 (x_hi: 2, x_lo: 2; x = x_hi * 2 + x_lo), y: 4, z: 8 (z_hi: 4, z_lo: 2; z = z_hi * 2 + z_lo), core: 2. Of those that a mesh axis runs over, the one named last changes fastest.
Arguments:
- fresh_keys: bfloat16 [32, 16384, 8, 128], P(None, ('block', 'span'), 'model'), may hold values from -6 to 6
- fresh_values: bfloat16 [32, 16384, 8, 128], P(None, ('block', 'span'), 'model'), may hold values from -6 to 6
- turn_angle: float32 [16384, 64], replicated, may hold values from -3.140625 to 3.140625
Outputs:
- decode_keys: bfloat16 [32, 8, 128, 16384], P(('block', 'span'), 'model')
- decode_values: bfloat16 [32, 16384, 8, 128], P(('block', 'span'), None, 'model')
- page_high: bfloat16 [32, 256, 8, 128], P(('block', 'span'), None, 'model')
- page_low: bfloat16 [32, 256, 8, 128], P(('block', 'span'), None, 'model')
All inputs are finite; a program needn't handle non-finite values.
Results may differ from a plain program's by a relative error of at most 0.001.
Values may be sent and summed in bfloat16 or wider, within the bound.
A program may use at most 128 MiB of HBM per device.

v0:
```python
import jax
import jax.numpy as jnp
from jax import lax
from jax.sharding import PartitionSpec as P

PAGE = 64


def apply_rotary(vectors, angle):
    half = vectors.shape[-1] // 2
    cosine, sine = (jnp.cos(angle)[None, :, None, :], jnp.sin(angle)[None, :, None, :])
    first, second = (vectors[..., :half], vectors[..., half:])
    return jnp.concatenate(
        [first * cosine - second * sine, second * cosine + first * sine], axis=-1
    )


def ready_to_store(plain_keys, angle):
    wide_keys = plain_keys.astype(jnp.float32)
    return apply_rotary(wide_keys, angle)


def body(fresh_keys, fresh_values, turn_angle):
    my_angles = lax.dynamic_slice_in_dim(
        turn_angle, lax.axis_index(("block", "span")) * fresh_keys.shape[1], fresh_keys.shape[1]
    )
    sent_keys = ready_to_store(fresh_keys, my_angles).astype(jnp.bfloat16)
    moved_keys, decode_values = (
        lax.all_to_all(sent_keys, ("block", "span"), split_axis=0, concat_axis=1, tiled=True),
        lax.all_to_all(fresh_values, ("block", "span"), split_axis=0, concat_axis=1, tiled=True),
    )
    page_view = moved_keys.reshape(
        moved_keys.shape[0], -1, PAGE, moved_keys.shape[2], moved_keys.shape[3]
    )
    page_high = jnp.max(page_view, axis=2)
    page_low = jnp.min(page_view, axis=2)
    decode_keys = jnp.transpose(moved_keys, (0, 2, 3, 1))
    return (decode_keys, decode_values, page_high, page_low)


def solution(mesh):
    placed = (
        P(None, ("block", "span"), "model", None),
        P(None, ("block", "span"), "model", None),
        P(),
    )
    return jax.shard_map(
        body,
        mesh=mesh,
        in_specs=placed,
        out_specs=(
            P(("block", "span"), "model", None, None),
            P(("block", "span"), None, "model", None),
            P(("block", "span"), None, "model", None),
            P(("block", "span"), None, "model", None),
        ),
        check_vma=False,
    )
```

profile of v0, /device:TPU:65, one launch (start us, length us, event | category | flops | bytes accessed | tf_op | source)
XLA Modules:
  0.0 218.1 jit_solution(14781370510084889283)
XLA Ops:
  0.6 1.4 dynamic-slice_cosine_fusion
  2.0 0.1 copy.7
  2.1 0.1 copy.8
  2.3 3.2 %convert_element_type.12 = f32[32,512,1,128]{3,1,2,0:T(8,128)S(1)} convert(bf16[32,512,1,128]{3,1,2,0:T(8,128)(2,1)} %param.3) | non-fusion elementwise | flops 2097152 | bytes 12582912 | tf_op jit(solution)/shard_map/convert_element_type | solution.py:19
  5.5 3.0 %subtract_convert_fusion = (bf16[32,512,1,64]{3,1,2,0:T(8,128)(2,1)S(1)}, bf16[32,512,1,64]{3,1,2,0:T(8,128)(2,1)S(1)}) fusion(f32[32,512,1,128]{3,1,2,0:T(8,128)S(1)} %convert_element_type.12, f32[512,64]{1,0:T(8,128)S(1)} %copy.8, f32[512,64]{1,0:T(8,128)S(1)} %copy.7), kind=kLoop, calls=%fused_computation.1 | loop fusion | flops 8388608 | bytes 12845056 | tf_op jit(solution)/shard_map/convert
  8.5 2.3 %pad_maximum_fusion = bf16[32,512,1,128]{3,1,2,0:T(8,128)(2,1)S(1)} fusion(bf16[32,512,1,64]{3,1,2,0:T(8,128)(2,1)S(1)} %get-tuple-element.7, bf16[32,512,1,64]{3,1,2,0:T(8,128)(2,1)S(1)} %get-tuple-element.6), kind=kLoop, calls=%fused_computation.2 | loop fusion | flops 8388608 | bytes 8388608 | tf_op jit(solution)/shard_map/concatenate | solution.py:13
  10.8 103.6 %all_to_all.24 = bf16[32,512,1,128]{3,1,2,0:T(8,128)(2,1)} all-to-all(bf16[32,512,1,128]{3,1,2,0:T(8,128)(2,1)S(1)} %pad_maximum_fusion), channel_id=1, replica_groups=mesh['block'=8,'span'=4,'model'=8] {'block','span'}, dimensions={0} | all-to-all | bytes 8388608 | tf_op jit(solution)/shard_map/all_to_all | solution.py:29
  114.4 5.7 %all-to-all-start.1 = ((bf16[32,512,1,128]{3,1,2,0:T(8,128)(2,1)}), bf16[32,512,1,128]{3,1,2,0:T(8,128)(2,1)}, u32[]{:S(2)}, u32[]{:S(2)}) async-start(bf16[32,512,1,128]{3,1,2,0:T(8,128)(2,1)} %param.4), calls=%async_computation.1 | async-start | bytes 8388608 | tf_op jit(solution)/shard_map/all_to_all | solution.py:30
  120.1 6.4 %copy.10 = bf16[1,16384,1,128]{1,3,2,0:T(8,128)(2,1)} copy(bf16[1,16384,1,128]{3,1,2,0:T(8,128)(2,1)} %bitcast.6) | data formatting | bytes 8388608 | tf_op jit(solution)/shard_map/all_to_all | solution.py:29
  126.5 5.6 %fusion = (bf16[256,128]{1,0:T(8,128)(2,1)}, bf16[256,128]{1,0:T(8,128)(2,1)}) fusion(bf16[1,256,64,1,128]{4,2,1,3,0:T(8,128)(2,1)} %bitcast.7), kind=kLoop, calls=%fused_computation.5 | loop fusion | flops 4128768 | bytes 4325376 | tf_op jit(solution)/shard_map/reduce_min | solution.py:36
  132.1 82.3 %all-to-all-done.1 = bf16[32,512,1,128]{3,1,2,0:T(8,128)(2,1)} async-done(((bf16[32,512,1,128]{3,1,2,0:T(8,128)(2,1)}), bf16[32,512,1,128]{3,1,2,0:T(8,128)(2,1)}, u32[]{:S(2)}, u32[]{:S(2)}) %all-to-all-start.1) | async-done | bytes 4194336 | tf_op jit(solution)/shard_map/all_to_all | solution.py:30
  214.4 3.7 %copy.12 = bf16[1,16384,1,128]{3,1,2,0:T(8,128)(2,1)} copy(bf16[1,16384,1,128]{3,1,2,0:T(8,128)(2,1)} %bitcast.2) | data formatting | bytes 8388608
Async XLA Ops:
  114.4 100.0 %all-to-all-start.1 = ((bf16[32,512,1,128]{3,1,2,0:T(8,128)(2,1)}), bf16[32,512,1,128]{3,1,2,0:T(8,128)(2,1)}, u32[]{:S(2)}, u32[]{:S(2)}) async-start(bf16[32,512,1,128]{3,1,2,0:T(8,128)(2,1)} %param.4), calls=%async_computation.1 | async-start | bytes 8388608 | tf_op jit(solution)/shard_map/all_to_all | solution.py:30
where the time goes:
time: 219 us; the launch traced here: 218 us
  blocking collectives  104 us (47%)
  waiting for transfers between devices  82.3 us (38%)
  other arithmetic  14.1 us (6%)
  local copies, waits for them, and re-layouts  11.7 us (5%)
  starting transfers between devices  5.69 us (3%)
    all_to_all x1, blocking collectives, body(): lax.all_to_all(sent_keys, ('block', 'span'), split_axis=0, concat_axis=1,...  104 us
    all_to_all x1, waiting for transfers between devices, body(): lax.all_to_all(fresh_values, ('block', 'span'), split_axis=0, concat_axis...  82.3 us
    all_to_all x1, local copies, waits for them, and re-layouts, body(): lax.all_to_all(sent_keys, ('block', 'span'), split_axis=0, concat_axis=1,...  6.37 us
    all_to_all x1, starting transfers between devices, body(): lax.all_to_all(fresh_values, ('block', 'span'), split_axis=0, concat_axis...  5.69 us
    reduce_min x1, other arithmetic, body(): page_low = jnp.min(page_view, axis=2)  5.58 us
  transfers between devices with their start and end apart: 1, of which 1 were waited for; matrix products, arithmetic and copies ran while one was open for 5% of the time, Pallas kernels for 0%

commit v1 on v0

v1 whole, which is shorter than its diff:
```python
import functools

import jax
import jax.numpy as jnp
from jax import lax
from jax.experimental import pallas as pl
from jax.experimental.pallas import tpu as pltpu
from jax.sharding import PartitionSpec as P

PAGE = 64
MESH = pl.DeviceIdType.MESH
RING = 8
STEPS = (1, 7, 2, 6, 3, 5, 4)
ALONG = tuple((dz, dc) for dz in STEPS for dc in range(2))


def place(core, x, z, model):
    return ((z % 2) * 4 + x * 2 + core, z // 2, model)


def rank(core, x, z):
    return ((z % 2) * 4 + x * 2 + core) * 4 + z // 2


def exchange(
    keys, values, angle, out_keys, out_values, out_high, out_low,
    plain, turned, landed, relay, angles, cosine, sine, high, low,
    load_sem, send_sem, recv_sem, pass_send_sem, pass_recv_sem,
):
    block, span, model = (lax.axis_index(a) for a in ("block", "span", "model"))
    core, x, z = block % 2, (block // 2) % 2, span * 2 + block // 4
    me = rank(core, x, z)
    count, rows, size = plain.shape
    pages = rows // PAGE
    half = size // 2

    def remote(src, dst, ssem, rsem, to):
        return pltpu.make_async_remote_copy(
            src, dst, ssem, rsem, device_id=place(*to, model), device_id_type=MESH
        )

    def rows_of(r):
        return pl.ds(pl.multiple_of(r * rows, rows), rows)

    barrier = pltpu.get_barrier_semaphore()
    peers = [((core + dc) % 2, x, (z + dz) % RING) for dz, dc in ALONG]
    mate = (1 - core, x, z)
    across = [(c, 1 - x, z) for c in (core, 1 - core)]
    for to in peers + [mate] + across:
        pl.semaphore_signal(barrier, inc=1, device_id=place(*to, model), device_id_type=MESH)

    get_angle = pltpu.make_async_copy(angle.at[:, rows_of(me)], angles, load_sem.at[0])
    get_angle.start()
    get_keys = pltpu.make_async_copy(keys, plain, load_sem.at[1])
    get_keys.start()
    put_own = pltpu.make_async_copy(values.at[me], out_values.at[rows_of(me)], load_sem.at[2])
    put_own.start()

    n = len(ALONG)
    def along(kind, i):
        to = peers[i]
        c2, _, z2 = to
        final = rank(c2, 1 - x if kind < 2 else x, z2)
        src = (values if kind in (0, 3) else turned).at[final]
        if kind < 2:
            dst = relay.at[kind, i]
        elif kind == 2:
            dst = landed.at[me]
        else:
            dst = out_values.at[rows_of(me)]
        return remote(src, dst, send_sem.at[kind * n + i], recv_sem.at[kind * n + i], to)

    def beside(i, what):
        to = ([mate] + across)[i]
        at = 4 * n + what * 3 + i
        src = (values if what == 0 else turned).at[rank(*to)]
        dst = out_values.at[rows_of(me)] if what == 0 else landed.at[me]
        return remote(src, dst, send_sem.at[at], recv_sem.at[at], to)

    def passed(kind, i):
        dz, dc = ALONG[i]
        origin = rank((core - dc) % 2, x, (z - dz) % RING)
        dst = out_values.at[rows_of(origin)] if kind == 0 else landed.at[origin]
        return remote(
            relay.at[kind, i], dst, pass_send_sem.at[kind * n + i], pass_recv_sem.at[kind * n + i],
            across[0],
        )

    get_angle.wait()
    a = angles[...]
    ca, sa = jnp.cos(a), jnp.sin(a)
    cosine[...] = jnp.concatenate([ca, ca], axis=0).T
    sine[...] = jnp.concatenate([-sa, sa], axis=0).T

    pl.semaphore_wait(barrier, n + 3)
    for i in range(n):
        along(0, i).start()
    for i in range(3):
        beside(i, 0).start()

    get_keys.wait()
    part = 128

    def turn(j, _):
        s = j // (rows // part)
        r = pl.ds(pl.multiple_of((j % (rows // part)) * part, part), part)
        v = plain[s, r, :].astype(jnp.float32)
        w = v * cosine[r, :] + pltpu.roll(v, half, 1) * sine[r, :]
        turned[s, r, :] = w.astype(jnp.bfloat16)
        return 0

    lax.fori_loop(0, count * (rows // part), turn, 0)

    def finish(ref, s, origin):
        v = ref[s]
        out_keys[:, rows_of(origin)] = v.T
        g = v.astype(jnp.float32).reshape(pages, PAGE, size)
        at = pl.ds(pl.multiple_of(origin * pages, pages), pages)
        high[at, :] = jnp.max(g, axis=1)
        low[at, :] = jnp.min(g, axis=1)

    finish(turned, me, me)
    for kind in (1, 2):
        for i in range(n):
            along(kind, i).start()
    for i in range(3):
        beside(i, 1).start()
    for i in range(n):
        along(3, i).start()

    for kind in (0, 1):
        for i in range(n):
            along(kind, i).wait_recv()
            passed(kind, i).start()

    def arrive(i, _):
        pass

    def origin_of(i, col):
        dz, dc = ALONG[i]
        return rank((core - dc) % 2, col, (z - dz) % RING)

    for i in range(3):
        beside(i, 1).wait_recv()
        finish(landed, rank(*([mate] + across)[i]), rank(*([mate] + across)[i]))
    for i in range(n):
        along(2, i).wait_recv()
        o = origin_of(i, x)
        finish(landed, o, o)
    for i in range(n):
        passed(1, i).wait_recv()
        o = origin_of(i, 1 - x)
        finish(landed, o, o)
    out_high[...] = high[...].astype(jnp.bfloat16)
    out_low[...] = low[...].astype(jnp.bfloat16)

    put_own.wait()
    for i in range(3):
        beside(i, 0).wait_recv()
    for i in range(n):
        passed(0, i).wait_recv()
    for i in range(n):
        along(3, i).wait_recv()
    for kind in range(4):
        for i in range(n):
            along(kind, i).wait_send()
    for what in range(2):
        for i in range(3):
            beside(i, what).wait_send()
    for kind in range(2):
        for i in range(n):
            passed(kind, i).wait_send()


def body(fresh_keys, fresh_values, turn_angle):
    count, rows, _, size = fresh_keys.shape
    length = count * rows
    n = len(ALONG)
    plain = (count, rows, size)
    vmem = pl.BlockSpec(memory_space=pltpu.VMEM)
    hbm = pl.BlockSpec(memory_space=pltpu.HBM)
    out = pl.pallas_call(
        exchange,
        out_shape=[
            jax.ShapeDtypeStruct((size, length), jnp.bfloat16),
            jax.ShapeDtypeStruct((length, size), jnp.bfloat16),
            jax.ShapeDtypeStruct((length // PAGE, size), jnp.bfloat16),
            jax.ShapeDtypeStruct((length // PAGE, size), jnp.bfloat16),
        ],
        in_specs=[hbm] * 3,
        out_specs=[vmem] * 4,
        scratch_shapes=[
            pltpu.VMEM(plain, jnp.bfloat16),
            pltpu.VMEM(plain, jnp.bfloat16),
            pltpu.VMEM(plain, jnp.bfloat16),
            pltpu.VMEM((2, n, rows, size), jnp.bfloat16),
            pltpu.VMEM((size // 2, rows), jnp.float32),
            pltpu.VMEM((rows, size), jnp.float32),
            pltpu.VMEM((rows, size), jnp.float32),
            pltpu.VMEM((length // PAGE, size), jnp.float32),
            pltpu.VMEM((length // PAGE, size), jnp.float32),
            pltpu.SemaphoreType.DMA((3,)),
            pltpu.SemaphoreType.DMA((4 * n + 6,)),
            pltpu.SemaphoreType.DMA((4 * n + 6,)),
            pltpu.SemaphoreType.DMA((2 * n,)),
            pltpu.SemaphoreType.DMA((2 * n,)),
        ],
        compiler_params=pltpu.CompilerParams(
            collective_id=0, has_side_effects=True, vmem_limit_bytes=36 << 20
        ),
        name="exchange",
    )(fresh_keys.reshape(plain), fresh_values.reshape(plain), turn_angle.T)
    keys, values, high, low = out
    return (
        keys[None, None],
        values.reshape(1, length, 1, size),
        high.reshape(1, length // PAGE, 1, size),
        low.reshape(1, length // PAGE, 1, size),
    )


def solution(mesh):
    placed = (
        P(None, ("block", "span"), "model", None),
        P(None, ("block", "span"), "model", None),
        P(),
    )
    return jax.shard_map(
        body,
        mesh=mesh,
        in_specs=placed,
        out_specs=(
            P(("block", "span"), "model", None, None),
            P(("block", "span"), None, "model", None),
            P(("block", "span"), None, "model", None),
            P(("block", "span"), None, "model", None),
        ),
        check_vma=False,
    )
```

time: 219 us -> 201 us (0.918)
  Pallas kernels: 0 us -> 189 us
  blocking collectives: 104 us -> 0 us
  waiting for transfers between devices: 82.3 us -> 0 us
  other arithmetic: 14.1 us -> 0 us
  starting transfers between devices: 5.69 us -> 0 us
    pallas_call x0 -> x1, Pallas kernels: none -> 189 us  [body(): pl.pallas_call(exchange, out_shape=[jax.ShapeDtypeStruct((size, length),...]
    all_to_all x1 -> x0, blocking collectives: 104 us -> none  [body(): lax.all_to_all(sent_keys, ('block', 'span'), split_axis=0, concat_axis=1,...]
    all_to_all x1 -> x0, waiting for transfers between devices: 82.3 us -> none  [body(): lax.all_to_all(fresh_values, ('block', 'span'), split_axis=0, concat_axis...]
    all_to_all x1 -> x0, local copies, waits for them, and re-layouts: 6.37 us -> none  [body(): lax.all_to_all(sent_keys, ('block', 'span'), split_axis=0, concat_axis=1,...]
    unnamed x1 -> x8, local copies, waits for them, and re-layouts: 3.74 us -> 9.65 us
    all_to_all x1 -> x0, starting transfers between devices: 5.69 us -> none  [body(): lax.all_to_all(fresh_values, ('block', 'span'), split_axis=0, concat_axis...]
    reduce_min x1 -> x0, other arithmetic: 5.58 us -> none  [body(): page_low = jnp.min(page_view, axis=2)]
    convert_element_type x1 -> x0, other arithmetic: 3.18 us -> none  [ready_to_store(): wide_keys = plain_keys.astype(jnp.float32)]
  transfers between devices with their start and end apart: 1 -> 0, of which waited for: 1 -> 0; matrix products, arithmetic and copies ran while one was open for 5% -> 0% of each run, Pallas kernels for 0% -> 0%
where the time goes in v1:
time: 201 us; the launch traced here: 200 us
  Pallas kernels  189 us (94%)
  local copies, waits for them, and re-layouts  9.65 us (5%)
    pallas_call x1, Pallas kernels, body(): pl.pallas_call(exchange, out_shape=[jax.ShapeDtypeStruct((size, length),...  189 us
    unnamed x8, local copies, waits for them, and re-layouts  9.65 us

profile of v1, /device:TPU:65, one launch (start us, length us, event | category | flops | bytes accessed | tf_op | source)
XLA Modules:
  0.0 199.7 jit_solution(10305059677722442476)
XLA Ops:
  0.6 0.0 copy-start
  0.6 2.2 %copy-done = bf16[32,512,1,128]{3,1,2,0:T(8,128)(2,1)S(1)} copy-done((bf16[32,512,1,128]{3,1,2,0:T(8,128)(2,1)S(1)}, bf16[32,512,1,128]{3,1,2,0:T(8,128)(2,1)}, u32[]{:S(2)}) %copy-start) | copy-done | bytes 4194328
  2.8 0.0 copy-start.1
  2.8 2.2 %copy-done.1 = bf16[32,512,1,128]{3,1,2,0:T(8,128)(2,1)S(1)} copy-done((bf16[32,512,1,128]{3,1,2,0:T(8,128)(2,1)S(1)}, bf16[32,512,1,128]{3,1,2,0:T(8,128)(2,1)}, u32[]{:S(2)}) %copy-start.1) | copy-done | bytes 4194328
  5.0 189.4 %exchange.1 = (bf16[128,16384]{1,0:T(8,128)(2,1)S(1)}, bf16[16384,128]{1,0:T(8,128)(2,1)S(1)}, bf16[256,128]{1,0:T(8,128)(2,1)S(1)}, bf16[256,128]{1,0:T(8,128)(2,1)S(1)}) custom-call(bf16[32,512,128]{2,1,0:T(8,128)(2,1)S(1)} %bitcast.7, bf16[32,512,128]{2,1,0:T(8,128)(2,1)S(1)} %bitcast.8, f32[64,16384]{1,0:T(8,128)} %bitcast.13), custom_call_target="tpu_custom_call" | custom-call | tf_op jit(solution)/shard_map/exchange/pallas_call | solution.py:182
  194.4 2.0 %copy.11 = bf16[1,1,128,16384]{3,2,1,0:T(8,128)(2,1)} copy(bf16[1,1,128,16384]{3,2,1,0:T(8,128)(2,1)S(1)} %bitcast.10) | data formatting | bytes 8388608
  196.4 2.0 %copy.12 = bf16[1,16384,1,128]{3,1,2,0:T(8,128)(2,1)} copy(bf16[1,16384,1,128]{3,1,2,0:T(8,128)(2,1)S(1)} %bitcast.9) | data formatting | bytes 8388608
  198.4 0.6 copy.13
  199.1 0.6 copy.14
Async XLA Ops:
  0.6 2.2 %copy-start = (bf16[32,512,1,128]{3,1,2,0:T(8,128)(2,1)S(1)}, bf16[32,512,1,128]{3,1,2,0:T(8,128)(2,1)}, u32[]{:S(2)}) copy-start(bf16[32,512,1,128]{3,1,2,0:T(8,128)(2,1)} %param.3) | copy-start | bytes 12582916
  2.8 2.2 %copy-start.1 = (bf16[32,512,1,128]{3,1,2,0:T(8,128)(2,1)S(1)}, bf16[32,512,1,128]{3,1,2,0:T(8,128)(2,1)}, u32[]{:S(2)}) copy-start(bf16[32,512,1,128]{3,1,2,0:T(8,128)(2,1)} %param.4) | copy-start | bytes 12582916

commit v2 on v1

--- a/solution.py
+++ b/solution.py
@@ -11,6 +11,7 @@
 MESH = pl.DeviceIdType.MESH
 RING = 8
 STEPS = (1, 7, 2, 6, 3, 5, 4)
+PIECES = (8, 8, 1, 1)
 ALONG = tuple((dz, dc) for dz in STEPS for dc in range(2))
 
 
@@ -133,9 +134,6 @@
             along(kind, i).wait_recv()
             passed(kind, i).start()
 
-    def arrive(i, _):
-        pass
-
     def origin_of(i, col):
         dz, dc = ALONG[i]
         return rank((core - dc) % 2, col, (z - dz) % RING)
@@ -170,6 +168,23 @@
     for kind in range(2):
         for i in range(n):
             passed(kind, i).wait_send()
+
+
+def store(*refs):
+    n = len(PIECES)
+    sources, targets, sem = refs[:n], refs[n : 2 * n], refs[2 * n]
+    copies = []
+    for src, dst, pieces in zip(sources, targets, PIECES):
+        rows = src.shape[0] // pieces
+        for p in range(pieces):
+            at = pl.ds(p * rows, rows)
+            copies.append(
+                pltpu.make_async_copy(src.at[at], dst.at[at], sem.at[len(copies)])
+            )
+    for c in copies:
+        c.start()
+    for c in copies:
+        c.wait()
 
 
 def body(fresh_keys, fresh_values, turn_angle):
@@ -206,11 +221,19 @@
             pltpu.SemaphoreType.DMA((2 * n,)),
         ],
         compiler_params=pltpu.CompilerParams(
-            collective_id=0, has_side_effects=True, vmem_limit_bytes=36 << 20
+            collective_id=0, has_side_effects=True, vmem_limit_bytes=44 << 20
         ),
         name="exchange",
     )(fresh_keys.reshape(plain), fresh_values.reshape(plain), turn_angle.T)
-    keys, values, high, low = out
+    keys, values, high, low = pl.pallas_call(
+        store,
+        out_shape=[jax.ShapeDtypeStruct(o.shape, o.dtype) for o in out],
+        in_specs=[vmem] * 4,
+        out_specs=[hbm] * 4,
+        scratch_shapes=[pltpu.SemaphoreType.DMA((sum(PIECES),))],
+        compiler_params=pltpu.CompilerParams(vmem_limit_bytes=1 << 20),
+        name="store",
+    )(*out)
     return (
         keys[None, None],
         values.reshape(1, length, 1, size),

time: 201 us -> 195 us (0.970)
  local copies, waits for them, and re-layouts: 9.65 us -> 0 us
  Pallas kernels: 189 us -> 193 us
    unnamed x8 -> x0, local copies, waits for them, and re-layouts: 9.65 us -> none
    pallas_call x0 -> x1, Pallas kernels: none -> 3.45 us  [body(): pl.pallas_call(store, out_shape=[jax.ShapeDtypeStruct(o.shape, o.dtype) f...]
where the time goes in v2:
time: 195 us; the launch traced here: 194 us
  Pallas kernels  193 us (99%)
    pallas_call x1, Pallas kernels, body(): pl.pallas_call(exchange, out_shape=[jax.ShapeDtypeStruct((size, length),...  190 us

profile of v2, /device:TPU:65, one launch (start us, length us, event | category | flops | bytes accessed | tf_op | source)
XLA Modules:
  0.0 194.1 jit_solution(17753204169082369809)
XLA Ops:
  0.6 190.0 %exchange.1 = (bf16[128,16384]{1,0:T(8,128)(2,1)S(1)}, bf16[16384,128]{1,0:T(8,128)(2,1)S(1)}, bf16[256,128]{1,0:T(8,128)(2,1)S(1)}, bf16[256,128]{1,0:T(8,128)(2,1)S(1)}) custom-call(bf16[32,512,128]{2,1,0:T(8,128)(2,1)} %bitcast.7, bf16[32,512,128]{2,1,0:T(8,128)(2,1)} %bitcast.8, f32[64,16384]{1,0:T(8,128)} %bitcast.9), custom_call_target="tpu_custom_call" | custom-call | tf_op jit(solution)/shard_map/exchange/pallas_call | solution.py:197
  190.6 3.5 %store.1 = (bf16[128,16384]{1,0:T(8,128)(2,1)}, bf16[16384,128]{1,0:T(8,128)(2,1)}, bf16[256,128]{1,0:T(8,128)(2,1)}, bf16[256,128]{1,0:T(8,128)(2,1)}) custom-call(bf16[128,16384]{1,0:T(8,128)(2,1)S(1)} %get-tuple-element.12.refs_0_, bf16[16384,128]{1,0:T(8,128)(2,1)S(1)} %get-tuple-element.13.refs_1_, bf16[256,128]{1,0:T(8,128)(2,1)S(1)} %get-tuple-element.14.refs_2_, ...), custom_call_target="tpu_custom_call" | custom-call | tf_op jit(solution)/shard_map/store/pallas_call | solution.py:228

commit v3 on v2

--- a/solution.py
+++ b/solution.py
@@ -12,6 +12,8 @@
 RING = 8
 STEPS = (1, 7, 2, 6, 3, 5, 4)
 PIECES = (8, 8, 1, 1)
+ORDERS = (None, (3, 5, 1, 7, 4, 2, 6), (3, 5, 1, 7, 4, 2, 6), (3, 5, 1, 7, 4, 2, 6))
+LAST = tuple(range(7))
 ALONG = tuple((dz, dc) for dz in STEPS for dc in range(2))
 
 
@@ -26,7 +28,7 @@
 def exchange(
     keys, values, angle, out_keys, out_values, out_high, out_low,
     plain, turned, landed, relay, angles, cosine, sine, high, low,
-    load_sem, send_sem, recv_sem, pass_send_sem, pass_recv_sem,
+    load_sem, send_sem, recv_sem, pass_send_sem, pass_recv_sem, last_sem, known,
 ):
     block, span, model = (lax.axis_index(a) for a in ("block", "span", "model"))
     core, x, z = block % 2, (block // 2) % 2, span * 2 + block // 4
@@ -43,12 +45,18 @@
     def rows_of(r):
         return pl.ds(pl.multiple_of(r * rows, rows), rows)
 
-    barrier = pltpu.get_barrier_semaphore()
     peers = [((core + dc) % 2, x, (z + dz) % RING) for dz, dc in ALONG]
     mate = (1 - core, x, z)
     across = [(c, 1 - x, z) for c in (core, 1 - core)]
-    for to in peers + [mate] + across:
-        pl.semaphore_signal(barrier, inc=1, device_id=place(*to, model), device_id_type=MESH)
+    ahead, behind = (core, x, (z + 1) % RING), (core, x, (z + RING - 1) % RING)
+
+    def signal(sem, to):
+        pl.semaphore_signal(sem, inc=1, device_id=place(*to, model), device_id_type=MESH)
+
+    barrier = pltpu.get_barrier_semaphore()
+    near = [to for to, (dz, _) in zip(peers, ALONG) if dz in (1, RING - 1)]
+    for to in near + [mate] + across:
+        signal(barrier, to)
 
     get_angle = pltpu.make_async_copy(angle.at[:, rows_of(me)], angles, load_sem.at[0])
     get_angle.start()
@@ -58,6 +66,10 @@
     put_own.start()
 
     n = len(ALONG)
+
+    def order(kind):
+        return [ALONG.index((dz, dc)) for dz in ORDERS[kind] for dc in range(2)]
+
     def along(kind, i):
         to = peers[i]
         c2, _, z2 = to
@@ -71,6 +83,19 @@
             dst = out_values.at[rows_of(me)]
         return remote(src, dst, send_sem.at[kind * n + i], recv_sem.at[kind * n + i], to)
 
+    def last(j, dc, receiving=False):
+        at = 3 * n
+        if receiving:
+            dz, dc = ALONG[j]
+            to, owner = mate, ((z - dz) % RING) * 2 + (core - dc) % 2
+        else:
+            c2, z2 = (core + dc) % 2, j + jnp.where(z <= j, 1, 0)
+            to, owner = (c2, x, z2), z * 2 + core
+        return remote(
+            values.at[rank(*to)], out_values.at[rows_of(me)],
+            send_sem.at[at + j * (1 if receiving else 2) + (0 if receiving else dc)], last_sem.at[owner], to,
+        )
+
     def beside(i, what):
         to = ([mate] + across)[i]
         at = 4 * n + what * 3 + i
@@ -87,17 +112,26 @@
             across[0],
         )
 
+    pl.semaphore_wait(barrier, len(near) + 3)
+    for i in range(3):
+        beside(i, 0).start()
+    for step in range(1, RING // 2 + 1):
+        for i, (dz, _) in enumerate(ALONG):
+            if dz in (step, RING - step):
+                along(0, i).start()
+        if step < RING // 2:
+            signal(known.at[step - 1, 0], ahead)
+            if step < RING // 2 - 1:
+                signal(known.at[step - 1, 1], behind)
+            pl.semaphore_wait(known.at[step - 1, 0], 1)
+            if step < RING // 2 - 1:
+                pl.semaphore_wait(known.at[step - 1, 1], 1)
+
     get_angle.wait()
     a = angles[...]
     ca, sa = jnp.cos(a), jnp.sin(a)
     cosine[...] = jnp.concatenate([ca, ca], axis=0).T
     sine[...] = jnp.concatenate([-sa, sa], axis=0).T
-
-    pl.semaphore_wait(barrier, n + 3)
-    for i in range(n):
-        along(0, i).start()
-    for i in range(3):
-        beside(i, 0).start()
 
     get_keys.wait()
     part = 128
@@ -121,13 +155,17 @@
         low[at, :] = jnp.min(g, axis=1)
 
     finish(turned, me, me)
-    for kind in (1, 2):
-        for i in range(n):
+    for kind in (1, 2, 3):
+        if kind == 3:
+            for j in LAST:
+                for dc in range(2):
+                    last(j, dc).start()
+            break
+        for i in order(kind):
             along(kind, i).start()
-    for i in range(3):
-        beside(i, 1).start()
-    for i in range(n):
-        along(3, i).start()
+        if kind == 2:
+            for i in range(3):
+                beside(i, 1).start()
 
     for kind in (0, 1):
         for i in range(n):
@@ -158,10 +196,13 @@
     for i in range(n):
         passed(0, i).wait_recv()
     for i in range(n):
-        along(3, i).wait_recv()
-    for kind in range(4):
+        last(i, 0, True).wait_recv()
+    for kind in range(3):
         for i in range(n):
             along(kind, i).wait_send()
+    for j in range(RING - 1):
+        for dc in range(2):
+            last(j, dc).wait_send()
     for what in range(2):
         for i in range(3):
             beside(i, what).wait_send()
@@ -219,6 +260,8 @@
             pltpu.SemaphoreType.DMA((4 * n + 6,)),
             pltpu.SemaphoreType.DMA((2 * n,)),
             pltpu.SemaphoreType.DMA((2 * n,)),
+            pltpu.SemaphoreType.DMA((2 * RING,)),
+            pltpu.SemaphoreType.REGULAR((RING // 2 - 1, 2)),
         ],
         compiler_params=pltpu.CompilerParams(
             collective_id=0, has_side_effects=True, vmem_limit_bytes=44 << 20

time: 195 us -> 194 us (level)
  no operation moved by 1% of the time
where the time goes in v3:
time: 194 us
  Pallas kernels  193 us (99%)
    pallas_call x1, Pallas kernels, body(): pl.pallas_call(exchange, out_shape=[jax.ShapeDtypeStruct((size, length),...  190 us

profile of v3, /device:TPU:65, one launch (start us, length us, event | category | flops | bytes accessed | tf_op | source)
XLA Modules:
  0.0 193.7 jit_solution(16042226275085804247)
XLA Ops:
  0.6 189.7 %exchange.1 = (bf16[128,16384]{1,0:T(8,128)(2,1)S(1)}, bf16[16384,128]{1,0:T(8,128)(2,1)S(1)}, bf16[256,128]{1,0:T(8,128)(2,1)S(1)}, bf16[256,128]{1,0:T(8,128)(2,1)S(1)}) custom-call(bf16[32,512,128]{2,1,0:T(8,128)(2,1)} %bitcast.7, bf16[32,512,128]{2,1,0:T(8,128)(2,1)} %bitcast.8, f32[64,16384]{1,0:T(8,128)} %bitcast.9), custom_call_target="tpu_custom_call" | custom-call | tf_op jit(solution)/shard_map/exchange/pallas_call | solution.py:238
  190.3 3.5 %store.1 = (bf16[128,16384]{1,0:T(8,128)(2,1)}, bf16[16384,128]{1,0:T(8,128)(2,1)}, bf16[256,128]{1,0:T(8,128)(2,1)}, bf16[256,128]{1,0:T(8,128)(2,1)}) custom-call(bf16[128,16384]{1,0:T(8,128)(2,1)S(1)} %get-tuple-element.12.refs_0_, bf16[16384,128]{1,0:T(8,128)(2,1)S(1)} %get-tuple-element.13.refs_1_, bf16[256,128]{1,0:T(8,128)(2,1)S(1)} %get-tuple-element.14.refs_2_, ...), custom_call_target="tpu_custom_call" | custom-call | tf_op jit(solution)/shard_map/store/pallas_call | solution.py:271

commit v4 on v2

v4 whole, which is shorter than its diff:
```python
import functools

import jax
import jax.numpy as jnp
from jax import lax
from jax.experimental import pallas as pl
from jax.experimental.pallas import tpu as pltpu
from jax.sharding import PartitionSpec as P

PAGE = 64
MESH = pl.DeviceIdType.MESH
RING = 8
PIECES = (4, 4, 1, 1)
EARLY = (1, 7, 2, 6, 3, 5, 4)
LATER = (3, 5, 1, 7, 4, 2, 6)
FINAL = (
    (7, 5, 6, 4, 3, 2, 1),
    (0, 4, 5, 7, 6, 2, 3),
    (0, 1, 6, 7, 5, 4, 3),
    (0, 1, 2, 7, 6, 5, 4),
    (1, 0, 2, 7, 3, 6, 5),
    (0, 1, 7, 2, 6, 3, 4),
    (0, 3, 1, 4, 2, 5, 7),
    (0, 3, 1, 4, 2, 5, 6),
)
ALONG = tuple((dz, dc) for dz in EARLY for dc in range(2))
PART = 128


def place(core, x, z, model):
    return ((z % 2) * 4 + x * 2 + core, z // 2, model)


def rank(core, x, z):
    return ((z % 2) * 4 + x * 2 + core) * 4 + z // 2


def exchange(
    keys, values, angle, out_keys, out_values, out_high, out_low,
    plain, turned, landed, relay, angles, cosine, sine, high, low,
    load_sem, send_sem, recv_sem, pass_send_sem, pass_recv_sem, last_send_sem, last_recv_sem,
    inside, known, staged, stage_sem,
):
    block, span, model = (lax.axis_index(a) for a in ("block", "span", "model"))
    core, x, z = block % 2, (block // 2) % 2, span * 2 + block // 4
    me = rank(core, x, z)
    count, rows, size = plain.shape
    pages = rows // PAGE
    half = size // 2
    n = len(ALONG)

    def remote(src, dst, ssem, rsem, to):
        return pltpu.make_async_remote_copy(
            src, dst, ssem, rsem, device_id=place(*to, model), device_id_type=MESH
        )

    def signal(sem, *devices):
        for to in devices:
            pl.semaphore_signal(sem, inc=1, device_id=place(*to, model), device_id_type=MESH)

    def rows_of(r):
        return pl.ds(pl.multiple_of(r * rows, rows), rows)

    peers = [((core + dc) % 2, x, (z + dz) % RING) for dz, dc in ALONG]
    mate = (1 - core, x, z)
    across = [(c, 1 - x, z) for c in (core, 1 - core)]
    ahead = [(c, x, (z + 1) % RING) for c in (core, 1 - core)]
    behind = [(c, x, (z + RING - 1) % RING) for c in (core, 1 - core)]

    def sends_to(dz):
        return [i for i, (d, _) in enumerate(ALONG) if d == dz]

    first_of_ahead = z <= 5
    first_of_behind = (z == 0) | (z == 7)
    first_of_across = x == 0
    first_of_mate = core == 1
    barrier = pltpu.get_barrier_semaphore()

    @pl.when(first_of_ahead)
    def _():
        signal(barrier, *ahead)

    @pl.when(first_of_behind)
    def _():
        signal(barrier, *behind)

    @pl.when(first_of_across)
    def _():
        signal(barrier, *across)

    @pl.when(first_of_mate)
    def _():
        signal(barrier, mate)

    def stage(side, i):
        c2, _, z2 = peers[i]
        return pltpu.make_async_copy(
            values.at[rank(c2, 1 - x, z2)], staged.at[side, ALONG[i][1]], stage_sem.at[side, ALONG[i][1]]
        )

    @pl.when(first_of_ahead)
    def _():
        for i in sends_to(1):
            stage(0, i).start()

    @pl.when(first_of_behind)
    def _():
        for i in sends_to(RING - 1):
            stage(1, i).start()

    get_angle = pltpu.make_async_copy(angle.at[:, rows_of(me)], angles, load_sem.at[0])
    get_angle.start()
    get_keys = pltpu.make_async_copy(keys, plain, load_sem.at[1])
    get_keys.start()
    put_own = pltpu.make_async_copy(values.at[me], out_values.at[rows_of(me)], load_sem.at[2])
    put_own.start()

    def along(kind, i, src=None):
        c2, _, z2 = to = peers[i]
        final = rank(c2, 1 - x if kind < 2 else x, z2)
        if src is None:
            src = (values if kind == 0 else turned).at[final]
        dst = relay.at[kind, i] if kind < 2 else landed.at[me]
        return remote(src, dst, send_sem.at[kind * n + i], recv_sem.at[kind * n + i], to)

    def beside(what, i):
        to = ([mate] + across)[i]
        at = 3 * n + what * 3 + i
        src = (values if what == 0 else turned).at[rank(*to)]
        dst = out_values.at[rows_of(me)] if what == 0 else landed.at[me]
        return remote(src, dst, send_sem.at[at], recv_sem.at[at], to)

    def origin(i, column):
        dz, dc = ALONG[i]
        return rank((core - dc) % 2, column, (z - dz) % RING)

    def passed(kind, i):
        dst = out_values.at[rows_of(origin(i, x))] if kind == 0 else landed.at[origin(i, x)]
        return remote(
            relay.at[kind, i], dst, pass_send_sem.at[kind * n + i], pass_recv_sem.at[kind * n + i],
            across[0],
        )


    def last(j, dc):
        to = ((core + dc) % 2, x, sum(jnp.where(z == k, t[j], 0) for k, t in enumerate(FINAL)))
        return remote(
            values.at[rank(*to)], out_values.at[rows_of(me)],
            last_send_sem.at[2 * j + dc], last_recv_sem.at[2 * z + core], to,
        )

    def last_from(i):
        dz, dc = ALONG[i]
        at = 2 * ((z - dz) % RING) + (core - dc) % 2
        src = out_values.at[rows_of(origin(i, x))]
        return remote(src, src, last_send_sem.at[0], last_recv_sem.at[at], peers[i])

    due = jnp.where(z == 6, 4, jnp.where(z == 0, 0, 2)) + 2 * x + 1 - core

    @pl.when(due > 0)
    def _():
        pl.semaphore_wait(barrier, due)

    def first_sends(dz):
        for i in sends_to(dz):
            along(0, i).start()

    def staged_sends(side, dz):
        for i in sends_to(dz):
            stage(side, i).wait()
            along(0, i, staged.at[side, ALONG[i][1]]).start()

    @pl.when(jnp.logical_not(first_of_behind))
    def _():
        first_sends(RING - 1)
        signal(inside.at[0], *behind)

    @pl.when(jnp.logical_not(first_of_ahead))
    def _():
        first_sends(1)
        signal(inside.at[1], *ahead)

    @pl.when(jnp.logical_not(first_of_across))
    def _():
        signal(inside.at[2], *across)

    @pl.when(jnp.logical_not(first_of_mate))
    def _():
        signal(inside.at[3], mate)

    @pl.when(first_of_ahead)
    def _():
        pl.semaphore_wait(inside.at[0], 2)
        staged_sends(0, 1)

    @pl.when(first_of_behind)
    def _():
        pl.semaphore_wait(inside.at[1], 2)
        staged_sends(1, RING - 1)

    far = RING // 2
    for step in range(1, far):
        signal(known.at[step - 1, 0], ahead[0])
        if step < far - 1:
            signal(known.at[step - 1, 1], behind[0])
        pl.semaphore_wait(known.at[step - 1, 0], 1)
        if step < far - 1:
            pl.semaphore_wait(known.at[step - 1, 1], 1)
        for dz in sorted({step + 1, RING - step - 1}):
            first_sends(dz)

    @pl.when(first_of_across)
    def _():
        pl.semaphore_wait(inside.at[2], 2)

    @pl.when(first_of_mate)
    def _():
        pl.semaphore_wait(inside.at[3], 1)

    for i in range(3):
        beside(0, i).start()

    get_angle.wait()
    a = angles[...]
    ca, sa = jnp.cos(a), jnp.sin(a)
    cosine[...] = jnp.concatenate([ca, ca], axis=0).T
    sine[...] = jnp.concatenate([-sa, sa], axis=0).T
    get_keys.wait()

    def turn(j, _):
        s = j // (rows // PART)
        r = pl.ds(pl.multiple_of((j % (rows // PART)) * PART, PART), PART)
        v = plain[s, r, :].astype(jnp.float32)
        w = v * cosine[r, :] + pltpu.roll(v, half, 1) * sine[r, :]
        turned[s, r, :] = w.astype(jnp.bfloat16)
        return 0

    lax.fori_loop(0, count * (rows // PART), turn, 0)

    def finish(ref, o):
        v = ref[o]
        out_keys[:, rows_of(o)] = v.T
        g = v.astype(jnp.float32).reshape(pages, PAGE, size)
        at = pl.ds(pl.multiple_of(o * pages, pages), pages)
        high[at, :] = jnp.max(g, axis=1)
        low[at, :] = jnp.min(g, axis=1)

    finish(turned, me)
    for kind in (1, 2):
        for dz in LATER:
            for dc in range(2):
                along(kind, ALONG.index((dz, dc))).start()
    for i in range(3):
        beside(1, i).start()
    for j in range(RING - 1):
        for dc in range(2):
            last(j, dc).start()

    for kind in (0, 1):
        for i in range(n):
            along(kind, i).wait_recv()
            passed(kind, i).start()
    for i in range(3):
        beside(1, i).wait_recv()
        finish(landed, rank(*([mate] + across)[i]))
    for i in range(n):
        along(2, i).wait_recv()
        finish(landed, origin(i, x))
    for i in range(n):
        passed(1, i).wait_recv()
        finish(landed, origin(i, 1 - x))
    out_high[...] = high[...].astype(jnp.bfloat16)
    out_low[...] = low[...].astype(jnp.bfloat16)

    put_own.wait()
    for i in range(3):
        beside(0, i).wait_recv()
        for what in range(2):
            beside(what, i).wait_send()
    for i in range(n):
        passed(0, i).wait_recv()
        for kind in range(2):
            passed(kind, i).wait_send()
        for kind in range(3):
            along(kind, i).wait_send()
    for i in range(n):
        last_from(i).wait_recv()
    for j in range(RING - 1):
        for dc in range(2):
            last(j, dc).wait_send()


def store(*refs):
    n = len(PIECES)
    sources, targets, sem = refs[:n], refs[n : 2 * n], refs[2 * n]
    copies = []
    for src, dst, pieces in zip(sources, targets, PIECES):
        rows = src.shape[0] // pieces
        for p in range(pieces):
            at = pl.ds(p * rows, rows)
            copies.append(
                pltpu.make_async_copy(src.at[at], dst.at[at], sem.at[len(copies)])
            )
    for c in copies:
        c.start()
    for c in copies:
        c.wait()


def body(fresh_keys, fresh_values, turn_angle):
    count, rows, _, size = fresh_keys.shape
    length = count * rows
    n = len(ALONG)
    plain = (count, rows, size)
    vmem = pl.BlockSpec(memory_space=pltpu.VMEM)
    hbm = pl.BlockSpec(memory_space=pl.ANY)
    dma = pltpu.SemaphoreType.DMA
    out = pl.pallas_call(
        exchange,
        out_shape=[
            jax.ShapeDtypeStruct((size, length), jnp.bfloat16),
            jax.ShapeDtypeStruct((length, size), jnp.bfloat16),
            jax.ShapeDtypeStruct((length // PAGE, size), jnp.bfloat16),
            jax.ShapeDtypeStruct((length // PAGE, size), jnp.bfloat16),
        ],
        in_specs=[hbm] * 3,
        out_specs=[vmem] * 4,
        scratch_shapes=[
            pltpu.VMEM(plain, jnp.bfloat16),
            pltpu.VMEM(plain, jnp.bfloat16),
            pltpu.VMEM(plain, jnp.bfloat16),
            pltpu.VMEM((2, n, rows, size), jnp.bfloat16),
            pltpu.VMEM((size // 2, rows), jnp.float32),
            pltpu.VMEM((rows, size), jnp.float32),
            pltpu.VMEM((rows, size), jnp.float32),
            pltpu.VMEM((length // PAGE, size), jnp.float32),
            pltpu.VMEM((length // PAGE, size), jnp.float32),
            dma((3,)),
            dma((3 * n + 6,)),
            dma((3 * n + 6,)),
            dma((2 * n,)),
            dma((2 * n,)),
            dma((n,)),
            dma((2 * RING,)),
            pltpu.SemaphoreType.REGULAR((4,)),
            pltpu.SemaphoreType.REGULAR((RING // 2 - 1, 2)),
            pltpu.VMEM((2, 2, rows, size), jnp.bfloat16),
            dma((2, 2)),
        ],
        compiler_params=pltpu.CompilerParams(
            collective_id=0, has_side_effects=True, vmem_limit_bytes=44 << 20
        ),
        name="exchange",
    )(fresh_keys.reshape(plain), fresh_values.reshape(plain), turn_angle.T)
    keys, values, high, low = pl.pallas_call(
        store,
        out_shape=[jax.ShapeDtypeStruct(o.shape, o.dtype) for o in out],
        in_specs=[vmem] * 4,
        out_specs=[hbm] * 4,
        scratch_shapes=[dma((sum(PIECES),))],
        compiler_params=pltpu.CompilerParams(vmem_limit_bytes=1 << 20),
        name="store",
    )(*out)
    return (
        keys[None, None],
        values.reshape(1, length, 1, size),
        high.reshape(1, length // PAGE, 1, size),
        low.reshape(1, length // PAGE, 1, size),
    )


def solution(mesh):
    placed = (
        P(None, ("block", "span"), "model", None),
        P(None, ("block", "span"), "model", None),
        P(),
    )
    return jax.shard_map(
        body,
        mesh=mesh,
        in_specs=placed,
        out_specs=(
            P(("block", "span"), "model", None, None),
            P(("block", "span"), None, "model", None),
            P(("block", "span"), None, "model", None),
            P(("block", "span"), None, "model", None),
        ),
        check_vma=False,
    )
```

time: 195 us -> 193 us (0.990)
  Pallas kernels: 193 us -> 191 us
    pallas_call x1, Pallas kernels: 190 us -> 188 us  [body(): pl.pallas_call(exchange, out_shape=[jax.ShapeDtypeStruct((size, length),...]
where the time goes in v4:
time: 193 us; the launch traced here: 192 us
  Pallas kernels  191 us (99%)
    pallas_call x1, Pallas kernels, body(): pl.pallas_call(exchange, out_shape=[jax.ShapeDtypeStruct((size, length),...  188 us

profile of v4, /device:TPU:65, one launch (start us, length us, event | category | flops | bytes accessed | tf_op | source)
XLA Modules:
  0.0 191.8 jit_solution(4716514536342664101)
XLA Ops:
  0.6 187.7 %exchange.1 = (bf16[128,16384]{1,0:T(8,128)(2,1)S(1)}, bf16[16384,128]{1,0:T(8,128)(2,1)S(1)}, bf16[256,128]{1,0:T(8,128)(2,1)S(1)}, bf16[256,128]{1,0:T(8,128)(2,1)S(1)}) custom-call(bf16[32,512,128]{2,1,0:T(8,128)(2,1)} %bitcast.7, bf16[32,512,128]{2,1,0:T(8,128)(2,1)} %bitcast.8, f32[64,16384]{1,0:T(8,128)} %bitcast.9), custom_call_target="tpu_custom_call" | custom-call | tf_op jit(solution)/shard_map/exchange/pallas_call | solution.py:318
  188.4 3.4 %store.1 = (bf16[128,16384]{1,0:T(8,128)(2,1)}, bf16[16384,128]{1,0:T(8,128)(2,1)}, bf16[256,128]{1,0:T(8,128)(2,1)}, bf16[256,128]{1,0:T(8,128)(2,1)}) custom-call(bf16[128,16384]{1,0:T(8,128)(2,1)S(1)} %get-tuple-element.12.refs_0_, bf16[16384,128]{1,0:T(8,128)(2,1)S(1)} %get-tuple-element.13.refs_1_, bf16[256,128]{1,0:T(8,128)(2,1)S(1)} %get-tuple-element.14.refs_2_, ...), custom_call_target="tpu_custom_call" | custom-call | tf_op jit(solution)/shard_map/store/pallas_call | solution.py:355

commit v5 on v4

--- a/solution.py
+++ b/solution.py
@@ -14,16 +14,17 @@
 EARLY = (1, 7, 2, 6, 3, 5, 4)
 LATER = (3, 5, 1, 7, 4, 2, 6)
 FINAL = (
-    (7, 5, 6, 4, 3, 2, 1),
-    (0, 4, 5, 7, 6, 2, 3),
-    (0, 1, 6, 7, 5, 4, 3),
-    (0, 1, 2, 7, 6, 5, 4),
-    (1, 0, 2, 7, 3, 6, 5),
-    (0, 1, 7, 2, 6, 3, 4),
-    (0, 3, 1, 4, 2, 5, 7),
-    (0, 3, 1, 4, 2, 5, 6),
+    (7, 5, 6, 3, 2, 1),
+    (0, 4, 7, 6, 2, 3),
+    (0, 1, 7, 5, 4, 3),
+    (0, 1, 2, 6, 5, 4),
+    (1, 2, 7, 3, 6, 5),
+    (0, 7, 2, 6, 3, 4),
+    (0, 3, 1, 4, 5, 7),
+    (0, 1, 4, 2, 5, 6),
 )
 ALONG = tuple((dz, dc) for dz in EARLY for dc in range(2))
+DETOUR = 256
 PART = 128
 
 
@@ -39,7 +40,7 @@
     keys, values, angle, out_keys, out_values, out_high, out_low,
     plain, turned, landed, relay, angles, cosine, sine, high, low,
     load_sem, send_sem, recv_sem, pass_send_sem, pass_recv_sem, last_send_sem, last_recv_sem,
-    inside, known, staged, stage_sem,
+    inside, known, staged, stage_sem, detour, far_send_sem, far_recv_sem,
 ):
     block, span, model = (lax.axis_index(a) for a in ("block", "span", "model"))
     core, x, z = block % 2, (block // 2) % 2, span * 2 + block // 4
@@ -147,6 +148,49 @@
         return remote(
             values.at[rank(*to)], out_values.at[rows_of(me)],
             last_send_sem.at[2 * j + dc], last_recv_sem.at[2 * z + core], to,
+        )
+
+    opposite = (z + RING // 2) % RING
+    goes_round = (z == 1) | (z == 6)
+    between = (z == 3) | (z == 4)
+    front, back = pl.ds(0, rows - DETOUR), pl.ds(rows - DETOUR, DETOUR)
+
+    def back_of(r):
+        return pl.ds(pl.multiple_of(r * rows + rows - DETOUR, DETOUR), DETOUR)
+
+    def over(part):
+        to = (1 - core if part == 0 else core, x, opposite)
+        src = values.at[rank(*to)]
+        if part == 0:
+            dst = out_values.at[rows_of(me)]
+        elif part == 1:
+            src, dst = src.at[front], out_values.at[pl.ds(pl.multiple_of(me * rows, rows), rows - DETOUR)]
+        else:
+            src, dst = src.at[back], out_values.at[back_of(me)]
+        return remote(src, dst, far_send_sem.at[part], far_recv_sem.at[part], to)
+
+    def over_from(part):
+        o = rank(1 - core if part == 0 else core, x, opposite)
+        if part == 0:
+            src = out_values.at[rows_of(o)]
+        elif part == 1:
+            src = out_values.at[pl.ds(pl.multiple_of(o * rows, rows), rows - DETOUR)]
+        else:
+            src = out_values.at[back_of(o)]
+        return remote(src, src, far_send_sem.at[part], far_recv_sem.at[part], (core, x, opposite))
+
+    def go_round():
+        final = rank(core, x, opposite)
+        return remote(
+            values.at[final, back], detour, far_send_sem.at[3], far_recv_sem.at[3],
+            (core, x, jnp.where(z == 6, 4, 3)),
+        )
+
+    def go_on():
+        o = rank(core, x, jnp.where(z == 4, 6, 1))
+        return remote(
+            detour, out_values.at[back_of(o)], far_send_sem.at[4], far_recv_sem.at[2],
+            (core, x, jnp.where(z == 4, 2, 5)),
         )
 
     def last_from(i):
@@ -209,6 +253,10 @@
         for dz in sorted({step + 1, RING - step - 1}):
             first_sends(dz)
 
+    @pl.when(goes_round)
+    def _():
+        go_round().start()
+
     @pl.when(first_of_across)
     def _():
         pl.semaphore_wait(inside.at[2], 2)
@@ -252,14 +300,29 @@
                 along(kind, ALONG.index((dz, dc))).start()
     for i in range(3):
         beside(1, i).start()
-    for j in range(RING - 1):
+    for i in range(n):
+        along(0, i).wait_recv()
+        passed(0, i).start()
+
+    @pl.when(between)
+    def _():
+        go_round().wait_recv()
+        go_on().start()
+
+    for part in (0, 1):
+        over(part).start()
+
+    @pl.when(jnp.logical_not(goes_round))
+    def _():
+        over(2).start()
+
+    for j in range(RING - 2):
         for dc in range(2):
             last(j, dc).start()
 
-    for kind in (0, 1):
-        for i in range(n):
-            along(kind, i).wait_recv()
-            passed(kind, i).start()
+    for i in range(n):
+        along(1, i).wait_recv()
+        passed(1, i).start()
     for i in range(3):
         beside(1, i).wait_recv()
         finish(landed, rank(*([mate] + across)[i]))
@@ -283,9 +346,26 @@
             passed(kind, i).wait_send()
         for kind in range(3):
             along(kind, i).wait_send()
-    for i in range(n):
-        last_from(i).wait_recv()
-    for j in range(RING - 1):
+    @pl.when(goes_round)
+    def _():
+        go_round().wait_send()
+
+    @pl.when(jnp.logical_not(goes_round))
+    def _():
+        over(2).wait_send()
+
+    @pl.when(between)
+    def _():
+        go_on().wait_send()
+
+    for part in (0, 1):
+        over(part).wait_send()
+    for part in (0, 1, 2):
+        over_from(part).wait_recv()
+    for i in range(n):
+        if ALONG[i][0] != RING // 2:
+            last_from(i).wait_recv()
+    for j in range(RING - 2):
         for dc in range(2):
             last(j, dc).wait_send()
 
@@ -340,12 +420,15 @@
             dma((3 * n + 6,)),
             dma((2 * n,)),
             dma((2 * n,)),
-            dma((n,)),
+            dma((2 * (RING - 2),)),
             dma((2 * RING,)),
             pltpu.SemaphoreType.REGULAR((4,)),
             pltpu.SemaphoreType.REGULAR((RING // 2 - 1, 2)),
             pltpu.VMEM((2, 2, rows, size), jnp.bfloat16),
             dma((2, 2)),
+            pltpu.VMEM((DETOUR, size), jnp.bfloat16),
+            dma((5,)),
+            dma((4,)),
         ],
         compiler_params=pltpu.CompilerParams(
             collective_id=0, has_side_effects=True, vmem_limit_bytes=44 << 20

time: 193 us -> 193 us (level)
  no operation moved by 1% of the time
where the time goes in v5:
time: 193 us; the launch traced here: 191 us
  Pallas kernels  190 us (98%)
    pallas_call x1, Pallas kernels, body(): pl.pallas_call(exchange, out_shape=[jax.ShapeDtypeStruct((size, length),...  187 us

profile of v5, /device:TPU:65, one launch (start us, length us, event | category | flops | bytes accessed | tf_op | source)
XLA Modules:
  0.0 190.6 jit_solution(13585496245610478091)
XLA Ops:
  0.6 186.6 %exchange.1 = (bf16[128,16384]{1,0:T(8,128)(2,1)S(1)}, bf16[16384,128]{1,0:T(8,128)(2,1)S(1)}, bf16[256,128]{1,0:T(8,128)(2,1)S(1)}, bf16[256,128]{1,0:T(8,128)(2,1)S(1)}) custom-call(bf16[32,512,128]{2,1,0:T(8,128)(2,1)} %bitcast.7, bf16[32,512,128]{2,1,0:T(8,128)(2,1)} %bitcast.8, f32[64,16384]{1,0:T(8,128)} %bitcast.9), custom_call_target="tpu_custom_call" | custom-call | tf_op jit(solution)/shard_map/exchange/pallas_call | solution.py:398
  187.2 3.4 %store.1 = (bf16[128,16384]{1,0:T(8,128)(2,1)}, bf16[16384,128]{1,0:T(8,128)(2,1)}, bf16[256,128]{1,0:T(8,128)(2,1)}, bf16[256,128]{1,0:T(8,128)(2,1)}) custom-call(bf16[128,16384]{1,0:T(8,128)(2,1)S(1)} %get-tuple-element.12.refs_0_, bf16[16384,128]{1,0:T(8,128)(2,1)S(1)} %get-tuple-element.13.refs_1_, bf16[256,128]{1,0:T(8,128)(2,1)S(1)} %get-tuple-element.14.refs_2_, ...), custom_call_target="tpu_custom_call" | custom-call | tf_op jit(solution)/shard_map/store/pallas_call | solution.py:438

commit v6 on v5

--- a/solution.py
+++ b/solution.py
@@ -24,7 +24,7 @@
     (0, 1, 4, 2, 5, 6),
 )
 ALONG = tuple((dz, dc) for dz in EARLY for dc in range(2))
-DETOUR = 256
+DETOUR = 192
 PART = 128
 
 
@@ -156,7 +156,7 @@
     front, back = pl.ds(0, rows - DETOUR), pl.ds(rows - DETOUR, DETOUR)
 
     def back_of(r):
-        return pl.ds(pl.multiple_of(r * rows + rows - DETOUR, DETOUR), DETOUR)
+        return pl.ds(pl.multiple_of(r * rows + rows - DETOUR, 64), DETOUR)
 
     def over(part):
         to = (1 - core if part == 0 else core, x, opposite)
@@ -309,16 +309,21 @@
         go_round().wait_recv()
         go_on().start()
 
-    for part in (0, 1):
-        over(part).start()
-
-    @pl.when(jnp.logical_not(goes_round))
-    def _():
-        over(2).start()
-
+    def overs(mine):
+        @pl.when(mine)
+        def _():
+            for part in (0, 1):
+                over(part).start()
+
+        @pl.when(mine & jnp.logical_not(goes_round))
+        def _():
+            over(2).start()
+
+    overs(z != 3)
     for j in range(RING - 2):
         for dc in range(2):
             last(j, dc).start()
+    overs(z == 3)
 
     for i in range(n):
         along(1, i).wait_recv()

time: 193 us -> 192 us (level)
  no operation moved by 1% of the time
where the time goes in v6:
time: 192 us; the launch traced here: 191 us
  Pallas kernels  190 us (99%)
    pallas_call x1, Pallas kernels, body(): pl.pallas_call(exchange, out_shape=[jax.ShapeDtypeStruct((size, length),...  187 us

profile of v6, /device:TPU:65, one launch (start us, length us, event | category | flops | bytes accessed | tf_op | source)
XLA Modules:
  0.0 190.7 jit_solution(5857205243487416387)
XLA Ops:
  0.6 186.7 %exchange.1 = (bf16[128,16384]{1,0:T(8,128)(2,1)S(1)}, bf16[16384,128]{1,0:T(8,128)(2,1)S(1)}, bf16[256,128]{1,0:T(8,128)(2,1)S(1)}, bf16[256,128]{1,0:T(8,128)(2,1)S(1)}) custom-call(bf16[32,512,128]{2,1,0:T(8,128)(2,1)} %bitcast.7, bf16[32,512,128]{2,1,0:T(8,128)(2,1)} %bitcast.8, f32[64,16384]{1,0:T(8,128)} %bitcast.9), custom_call_target="tpu_custom_call" | custom-call | tf_op jit(solution)/shard_map/exchange/pallas_call | solution.py:403
  187.3 3.4 %store.1 = (bf16[128,16384]{1,0:T(8,128)(2,1)}, bf16[16384,128]{1,0:T(8,128)(2,1)}, bf16[256,128]{1,0:T(8,128)(2,1)}, bf16[256,128]{1,0:T(8,128)(2,1)}) custom-call(bf16[128,16384]{1,0:T(8,128)(2,1)S(1)} %get-tuple-element.12.refs_0_, bf16[16384,128]{1,0:T(8,128)(2,1)S(1)} %get-tuple-element.13.refs_1_, bf16[256,128]{1,0:T(8,128)(2,1)S(1)} %get-tuple-element.14.refs_2_, ...), custom_call_target="tpu_custom_call" | custom-call | tf_op jit(solution)/shard_map/store/pallas_call | solution.py:443

commit v7 on v6

--- a/solution.py
+++ b/solution.py
@@ -40,7 +40,7 @@
     keys, values, angle, out_keys, out_values, out_high, out_low,
     plain, turned, landed, relay, angles, cosine, sine, high, low,
     load_sem, send_sem, recv_sem, pass_send_sem, pass_recv_sem, last_send_sem, last_recv_sem,
-    inside, known, staged, stage_sem, detour, far_send_sem, far_recv_sem,
+    inside, known, by_way, staged, stage_sem, detour, far_send_sem, far_recv_sem,
 ):
     block, span, model = (lax.axis_index(a) for a in ("block", "span", "model"))
     core, x, z = block % 2, (block // 2) % 2, span * 2 + block // 4
@@ -73,7 +73,10 @@
 
     first_of_ahead = z <= 5
     first_of_behind = (z == 0) | (z == 7)
-    first_of_across = x == 0
+    leaf = (z == 4) | (z == 7)
+    hub = (z == 3) | (z == 0)
+    first_of_across = (x == 0) & jnp.logical_not(leaf)
+    second_of_across = (x == 1) & jnp.logical_not(leaf)
     first_of_mate = core == 1
     barrier = pltpu.get_barrier_semaphore()
 
@@ -199,7 +202,7 @@
         src = out_values.at[rows_of(origin(i, x))]
         return remote(src, src, last_send_sem.at[0], last_recv_sem.at[at], peers[i])
 
-    due = jnp.where(z == 6, 4, jnp.where(z == 0, 0, 2)) + 2 * x + 1 - core
+    due = jnp.where(z == 6, 4, jnp.where(z == 0, 0, 2)) + jnp.where(leaf, 0, 2 * x) + 1 - core
 
     @pl.when(due > 0)
     def _():
@@ -224,7 +227,7 @@
         first_sends(1)
         signal(inside.at[1], *ahead)
 
-    @pl.when(jnp.logical_not(first_of_across))
+    @pl.when(second_of_across)
     def _():
         signal(inside.at[2], *across)
 
@@ -260,6 +263,16 @@
     @pl.when(first_of_across)
     def _():
         pl.semaphore_wait(inside.at[2], 2)
+
+    @pl.when(hub)
+    def _():
+        signal(by_way.at[0], across[0])
+        pl.semaphore_wait(by_way.at[0], 1)
+        signal(by_way.at[1], (core, x, jnp.where(z == 0, 7, 4)))
+
+    @pl.when(leaf)
+    def _():
+        pl.semaphore_wait(by_way.at[1], 1)
 
     @pl.when(first_of_mate)
     def _():
@@ -429,6 +442,7 @@
             dma((2 * RING,)),
             pltpu.SemaphoreType.REGULAR((4,)),
             pltpu.SemaphoreType.REGULAR((RING // 2 - 1, 2)),
+            pltpu.SemaphoreType.REGULAR((2,)),
             pltpu.VMEM((2, 2, rows, size), jnp.bfloat16),
             dma((2, 2)),
             pltpu.VMEM((DETOUR, size), jnp.bfloat16),

time: 192 us -> 191 us (level)
  no operation moved by 1% of the time
where the time goes in v7:
time: 191 us
  Pallas kernels  190 us (99%)
    pallas_call x1, Pallas kernels, body(): pl.pallas_call(exchange, out_shape=[jax.ShapeDtypeStruct((size, length),...  187 us

profile of v7, /device:TPU:65, one launch (start us, length us, event | category | flops | bytes accessed | tf_op | source)
XLA Modules:
  0.0 190.8 jit_solution(434710986284607557)
XLA Ops:
  0.6 186.7 %exchange.1 = (bf16[128,16384]{1,0:T(8,128)(2,1)S(1)}, bf16[16384,128]{1,0:T(8,128)(2,1)S(1)}, bf16[256,128]{1,0:T(8,128)(2,1)S(1)}, bf16[256,128]{1,0:T(8,128)(2,1)S(1)}) custom-call(bf16[32,512,128]{2,1,0:T(8,128)(2,1)} %bitcast.7, bf16[32,512,128]{2,1,0:T(8,128)(2,1)} %bitcast.8, f32[64,16384]{1,0:T(8,128)} %bitcast.9), custom_call_target="tpu_custom_call" | custom-call | tf_op jit(solution)/shard_map/exchange/pallas_call | solution.py:416
  187.4 3.4 %store.1 = (bf16[128,16384]{1,0:T(8,128)(2,1)}, bf16[16384,128]{1,0:T(8,128)(2,1)}, bf16[256,128]{1,0:T(8,128)(2,1)}, bf16[256,128]{1,0:T(8,128)(2,1)}) custom-call(bf16[128,16384]{1,0:T(8,128)(2,1)S(1)} %get-tuple-element.12.refs_0_, bf16[16384,128]{1,0:T(8,128)(2,1)S(1)} %get-tuple-element.13.refs_1_, bf16[256,128]{1,0:T(8,128)(2,1)S(1)} %get-tuple-element.14.refs_2_, ...), custom_call_target="tpu_custom_call" | custom-call | tf_op jit(solution)/shard_map/store/pallas_call | solution.py:457

commit v8 on v7

--- a/solution.py
+++ b/solution.py
@@ -102,23 +102,6 @@
             values.at[rank(c2, 1 - x, z2)], staged.at[side, ALONG[i][1]], stage_sem.at[side, ALONG[i][1]]
         )
 
-    @pl.when(first_of_ahead)
-    def _():
-        for i in sends_to(1):
-            stage(0, i).start()
-
-    @pl.when(first_of_behind)
-    def _():
-        for i in sends_to(RING - 1):
-            stage(1, i).start()
-
-    get_angle = pltpu.make_async_copy(angle.at[:, rows_of(me)], angles, load_sem.at[0])
-    get_angle.start()
-    get_keys = pltpu.make_async_copy(keys, plain, load_sem.at[1])
-    get_keys.start()
-    put_own = pltpu.make_async_copy(values.at[me], out_values.at[rows_of(me)], load_sem.at[2])
-    put_own.start()
-
     def along(kind, i, src=None):
         c2, _, z2 = to = peers[i]
         final = rank(c2, 1 - x if kind < 2 else x, z2)
@@ -234,6 +217,23 @@
     @pl.when(jnp.logical_not(first_of_mate))
     def _():
         signal(inside.at[3], mate)
+
+    @pl.when(first_of_ahead)
+    def _():
+        for i in sends_to(1):
+            stage(0, i).start()
+
+    @pl.when(first_of_behind)
+    def _():
+        for i in sends_to(RING - 1):
+            stage(1, i).start()
+
+    get_angle = pltpu.make_async_copy(angle.at[:, rows_of(me)], angles, load_sem.at[0])
+    get_angle.start()
+    get_keys = pltpu.make_async_copy(keys, plain, load_sem.at[1])
+    get_keys.start()
+    put_own = pltpu.make_async_copy(values.at[me], out_values.at[rows_of(me)], load_sem.at[2])
+    put_own.start()
 
     @pl.when(first_of_ahead)
     def _():

time: 191 us -> 191 us (level)
  no operation moved by 1% of the time
where the time goes in v8:
time: 191 us
  Pallas kernels  190 us (99%)
    pallas_call x1, Pallas kernels, body(): pl.pallas_call(exchange, out_shape=[jax.ShapeDtypeStruct((size, length),...  187 us

profile of v8, /device:TPU:65, one launch (start us, length us, event | category | flops | bytes accessed | tf_op | source)
XLA Modules:
  0.0 190.7 jit_solution(15057839240080879772)
XLA Ops:
  0.6 186.7 %exchange.1 = (bf16[128,16384]{1,0:T(8,128)(2,1)S(1)}, bf16[16384,128]{1,0:T(8,128)(2,1)S(1)}, bf16[256,128]{1,0:T(8,128)(2,1)S(1)}, bf16[256,128]{1,0:T(8,128)(2,1)S(1)}) custom-call(bf16[32,512,128]{2,1,0:T(8,128)(2,1)} %bitcast.7, bf16[32,512,128]{2,1,0:T(8,128)(2,1)} %bitcast.8, f32[64,16384]{1,0:T(8,128)} %bitcast.9), custom_call_target="tpu_custom_call" | custom-call | tf_op jit(solution)/shard_map/exchange/pallas_call | solution.py:416
  187.3 3.4 %store.1 = (bf16[128,16384]{1,0:T(8,128)(2,1)}, bf16[16384,128]{1,0:T(8,128)(2,1)}, bf16[256,128]{1,0:T(8,128)(2,1)}, bf16[256,128]{1,0:T(8,128)(2,1)}) custom-call(bf16[128,16384]{1,0:T(8,128)(2,1)S(1)} %get-tuple-element.12.refs_0_, bf16[16384,128]{1,0:T(8,128)(2,1)S(1)} %get-tuple-element.13.refs_1_, bf16[256,128]{1,0:T(8,128)(2,1)S(1)} %get-tuple-element.14.refs_2_, ...), custom_call_target="tpu_custom_call" | custom-call | tf_op jit(solution)/shard_map/store/pallas_call | solution.py:457
